TPU v7x, 8 devices: a whole 2x2x1 slice. The times are simulated.
8 devices in a mesh: dp: 1 (over z), tp: 2 (over y), cp: 4 (over x, core).
Axes of the slice: x: 2, y: 2, z: 1, core: 2. Of those that a mesh axis runs over, the one named last changes fastest.
Arguments:
- hidden: bfloat16 [1024, 6144], P(('dp', 'cp'))
- seg_ids: int32 [1024], P(('dp', 'cp'))
- w_q: bfloat16 [6144, 6144], P(None, 'tp')
- b_q: bfloat16 [6144], P('tp')
- w_kv: bfloat16 [6144, 256], replicated
- b_kv: bfloat16 [256], replicated
- w_o: bfloat16 [6144, 6144], P('tp')
- b_o: bfloat16 [6144], replicated
- ln_gain: bfloat16 [6144], replicated
- ln_bias: bfloat16 [6144], replicated
Outputs:
- output 1: bfloat16 [1024, 6144], P(('dp', 'cp'))
- output 2: bfloat16 [1024, 128], P(('dp', 'cp'))
- output 3: bfloat16 [1024, 128], P(('dp', 'cp'))
All inputs are finite; a program needn't handle non-finite values.
Results may differ from a plain program's by a relative error of at most 0.0118747.
Values are sent between devices in bfloat16 or wider.
A program may use at most 1 GiB of HBM per device.

v0:
```python
import jax
import jax.numpy as jnp
from jax import lax
from jax.sharding import PartitionSpec as P, NamedSharding

HEAD_DIM = 128
LN_EPS = 1e-5
ATTN_SCALE = HEAD_DIM ** -0.5


def layer_norm(x_blk, ln_gain, ln_bias):
    x_float = x_blk.astype(jnp.float32)
    centered = x_float - jnp.mean(x_float, axis=-1, keepdims=True)
    variance = jnp.mean(centered * centered, axis=-1, keepdims=True)
    return (centered * lax.rsqrt(variance + LN_EPS) * ln_gain.astype(jnp.float32) + ln_bias.astype(jnp.float32)).astype(jnp.bfloat16)


def merge_block(q_blk, k_blk, v_float, visible, m_prev, l_prev, acc_prev):
    scores = jnp.einsum('bhd,kd->bhk', q_blk, k_blk, preferred_element_type=jnp.float32) * ATTN_SCALE
    scores = jnp.where(visible[:, None, :], scores, -jnp.inf)
    m_new = jnp.maximum(m_prev, jnp.max(scores, axis=-1))
    p_weights = jnp.exp(scores - m_new[..., None])
    rescale = jnp.exp(m_prev - m_new)
    l_new = l_prev * rescale + jnp.sum(p_weights, axis=-1)
    acc_new = acc_prev * rescale[..., None] + jnp.einsum('bhk,kd->bhd', p_weights, v_float, preferred_element_type=jnp.float32)
    return m_new, l_new, acc_new


def solution(mesh):
    n_cp = mesh.shape['cp']
    send_pairs = [(i, i + 1) for i in range(n_cp - 1)]

    def local_block(hidden, seg_ids, w_q, b_q, w_kv, b_kv, w_o, b_o, ln_gain, ln_bias):
        tok_local = hidden.shape[0]
        heads_loc = w_q.shape[1] // HEAD_DIM
        q_rows = min(tok_local, 128)
        n_qblk = tok_local // q_rows
        normed = layer_norm(hidden, ln_gain, ln_bias)
        q_all = (jnp.dot(normed, w_q, preferred_element_type=jnp.float32) + b_q.astype(jnp.float32)).astype(jnp.bfloat16)
        kv_own = (jnp.dot(normed, w_kv, preferred_element_type=jnp.float32) + b_kv.astype(jnp.float32)).astype(jnp.bfloat16)
        q_blocks = q_all.reshape(n_qblk, q_rows, heads_loc, HEAD_DIM)
        seg_blocks = seg_ids.reshape(n_qblk, q_rows)
        pos_local = jnp.arange(tok_local, dtype=jnp.int32)
        pos_blocks = pos_local.reshape(n_qblk, q_rows)
        my_index = lax.axis_index('cp')

        def sweep_keys(kv_blk, seg_keys, causal, is_valid, soft_state):
            k_blk = kv_blk[:, :HEAD_DIM]
            v_float = kv_blk[:, HEAD_DIM:].astype(jnp.float32)

            def one_block(block_in):
                q_blk, seg_q, pos_q, m_prev, l_prev, acc_prev = block_in
                visible = (seg_keys[None, :] == seg_q[:, None]) & is_valid
                if causal:
                    visible = visible & (pos_local[None, :] <= pos_q[:, None])
                return merge_block(q_blk, k_blk, v_float, visible, m_prev, l_prev, acc_prev)

            return tuple(lax.map(one_block, (q_blocks, seg_blocks, pos_blocks) + tuple(soft_state)))

        m_init = jnp.full((n_qblk, q_rows, heads_loc), -1e30, jnp.float32)
        l_init = jnp.zeros((n_qblk, q_rows, heads_loc), jnp.float32)
        acc_init = jnp.zeros((n_qblk, q_rows, heads_loc, HEAD_DIM), jnp.float32)
        own_state = sweep_keys(kv_own, seg_ids, True, True, (m_init, l_init, acc_init))

        def shift_step(step_idx, loop_carry):
            kv_blk, seg_keys, m_prev, l_prev, acc_prev = loop_carry
            kv_blk = lax.ppermute(kv_blk, 'cp', send_pairs)
            seg_keys = lax.ppermute(seg_keys, 'cp', send_pairs)
            new_state = sweep_keys(kv_blk, seg_keys, False, my_index >= step_idx, (m_prev, l_prev, acc_prev))
            return (kv_blk, seg_keys) + new_state

        loop_out = lax.fori_loop(1, n_cp, shift_step, (kv_own, seg_ids) + own_state)
        attn_out = (loop_out[4] / loop_out[3][..., None]).astype(jnp.bfloat16).reshape(tok_local, heads_loc * HEAD_DIM)
        partial = jnp.dot(attn_out, w_o, preferred_element_type=jnp.float32).astype(jnp.bfloat16)
        proj_sum = lax.psum(partial, 'tp')
        y_out = (hidden.astype(jnp.float32) + proj_sum.astype(jnp.float32) + b_o.astype(jnp.float32)).astype(jnp.bfloat16)
        return y_out, kv_own[:, :HEAD_DIM], kv_own[:, HEAD_DIM:]

    row_spec = P(('dp', 'cp'), None)
    tok_spec = P(('dp', 'cp'))
    mapped = jax.shard_map(local_block, mesh=mesh,
                           in_specs=(row_spec, tok_spec, P(None, 'tp'), P('tp'), P(None, None), P(None), P('tp', None), P(None), P(None), P(None)),
                           out_specs=(row_spec, row_spec, row_spec), check_vma=False)
    return mapped
```

profile of v0, /device:TPU:2, one launch (start us, length us, event | category | flops | bytes accessed | tf_op | source)
XLA Modules:
  0.0 227.0 jit_solution(11321464559900924612)
XLA Ops:
  7.3 0.8 convert_element_type.54
  8.1 1.0 convert_element_type.52
  9.1 0.7 convert_element_type.51
  9.8 2.4 %convert_reduce_fusion = f32[256]{0:T(256)S(1)} fusion(bf16[256,6144]{1,0:T(8,128)(2,1)} %param.16), kind=kLoop, calls=%fused_computation.67 | loop fusion | flops 3145472 | bytes 3146752 | tf_op jit(solution)/shard_map/reduce_sum | solution.py:13
  12.3 1.0 fusion.45
  13.3 18.7 %fusion.54 = bf16[32,8,24,128]{3,1,2,0:T(8,128)(2,1)} fusion(f32[3072]{0:T(1024)S(1)} %convert_element_type.56, bf16[6144,3072]{1,0:T(8,128)(2,1)} %param.18, bf16[256,6144]{1,0:T(8,128)(2,1)} %param.16, f32[6144]{0:T(1024)S(1)} %convert_element_type.52, f32[6144]{0:T(1024)S(1)} %convert_element_type.51, f32[256]{0:T(256)S(1)} %add_rsqrt_fusion, ...), kind=kOutput, calls=%fused_computation.82 | convolution fusion | flops 9674686464 | bytes 42530816 | tf_op jit(solution)/shard_map/dot_general | solution.py:39
  32.0 1.9 copy.18
  33.9 1.5 copy.15
  35.4 1.4 fusion.55
  36.8 13.1 %while.67 = (s32[]{:T(128)}, f32[2,128,24]{1,2,0:T(8,128)S(1)}, f32[2,128,24]{1,2,0:T(8,128)S(1)}, f32[2,128,24,128]{3,1,2,0:T(8,128)}, s32[256]{0:T(256)S(1)}, ...) while((s32[]{:T(128)}, f32[2,128,24]{1,2,0:T(8,128)S(1)}, ...), condition=%wide.region_5.6_spmd.clone, body=%wide.region_2.5_spmd.clone.sunk | while | flops 411024384 | bytes 37376188 | solution.py:58
  37.0 2.0 fusion.80
  39.0 1.3 fusion.81
  40.3 1.4 bitcast_dynamic-update-slice_fusion.5
  41.7 1.7 copy-done.3
  43.5 2.0 fusion.80
  45.5 1.3 fusion.81
  46.9 1.4 bitcast_dynamic-update-slice_fusion.5
  48.3 1.7 copy-done.3
  49.9 0.6 copy-done.8
  50.6 61.0 %while.66 = (s32[]{:T(128)}, bf16[256,256]{1,0:T(8,128)(2,1)S(1)}, s32[256]{0:T(256)S(1)}, f32[2,128,24]{1,2,0:T(8,128)S(1)}, f32[2,128,24]{1,2,0:T(8,128)S(1)},...) while((s32[]{:T(128)}, bf16[256,256]{1,0:T(8,128)(2,1)S(1)}, ...), condition=%wide.region_11.12_spmd, body=%wide.region_6.11_spmd.sunk | while | flops 411381760 | bytes 43185136 | solution.py:72
  50.6 1.9 collective-permute-start
  52.5 1.9 collective-permute-start.1
  54.4 3.0 %collective-permute-done.1 = s32[256]{0:T(256)S(1)} collective-permute-done((s32[256]{0:T(256)S(1)}, s32[256]{0:T(256)S(1)}, u32[]{:S(2)}, u32[]{:S(2)}) %collective-permute-start.1) | collective-permute-done | bytes 1056 | tf_op jit(solution)/shard_map/while/body/eval_jaxpr/ppermute | solution.py:68
  57.4 13.5 %while.68 = (s32[]{:T(128)}, f32[2,128,24]{1,2,0:T(8,128)S(1)}, f32[2,128,24]{1,2,0:T(8,128)S(1)}, f32[2,128,24,128]{3,1,2,0:T(8,128)}, s32[256]{0:T(256)S(1)}, ...) while((s32[]{:T(128)}, f32[2,128,24]{1,2,0:T(8,128)S(1)}, ...), condition=%wide.region_10.10_spmd.clone, body=%wide.region_7.9_spmd.clone.sunk | while | flops 411381760 | bytes 42130116 | solution.py:58
  57.6 2.0 fusion.85
  59.6 1.3 fusion.87
  61.1 1.4 bitcast_dynamic-update-slice_fusion.6
  62.5 1.7 copy-done.5
  64.3 2.0 fusion.85
  66.3 1.3 fusion.87
  67.7 0.2 constant_dynamic-slice_fusion.5
  67.8 1.4 bitcast_dynamic-update-slice_fusion.6
  69.2 1.7 copy-done.5
  70.9 1.9 collective-permute-start
  72.8 1.9 collective-permute-start.1
  74.8 3.0 %collective-permute-done.1 = s32[256]{0:T(256)S(1)} collective-permute-done((s32[256]{0:T(256)S(1)}, s32[256]{0:T(256)S(1)}, u32[]{:S(2)}, u32[]{:S(2)}) %collective-permute-start.1) | collective-permute-done | bytes 1056 | tf_op jit(solution)/shard_map/while/body/eval_jaxpr/ppermute | solution.py:68
  77.8 13.5 %while.68 = (s32[]{:T(128)}, f32[2,128,24]{1,2,0:T(8,128)S(1)}, f32[2,128,24]{1,2,0:T(8,128)S(1)}, f32[2,128,24,128]{3,1,2,0:T(8,128)}, s32[256]{0:T(256)S(1)}, ...) while((s32[]{:T(128)}, f32[2,128,24]{1,2,0:T(8,128)S(1)}, ...), condition=%wide.region_10.10_spmd.clone, body=%wide.region_7.9_spmd.clone.sunk | while | flops 411381760 | bytes 42130116 | solution.py:58
  77.9 2.0 fusion.85
  79.9 1.3 fusion.87
  81.3 0.2 constant_dynamic-slice_fusion.5
  81.4 1.4 bitcast_dynamic-update-slice_fusion.6
  82.9 1.7 copy-done.5
  84.6 2.0 fusion.85
  86.6 1.3 fusion.87
  88.2 1.4 bitcast_dynamic-update-slice_fusion.6
  89.6 1.7 copy-done.5
  91.3 1.9 collective-permute-start
  93.2 1.9 collective-permute-start.1
  95.1 3.0 %collective-permute-done.1 = s32[256]{0:T(256)S(1)} collective-permute-done((s32[256]{0:T(256)S(1)}, s32[256]{0:T(256)S(1)}, u32[]{:S(2)}, u32[]{:S(2)}) %collective-permute-start.1) | collective-permute-done | bytes 1056 | tf_op jit(solution)/shard_map/while/body/eval_jaxpr/ppermute | solution.py:68
  98.1 13.5 %while.68 = (s32[]{:T(128)}, f32[2,128,24]{1,2,0:T(8,128)S(1)}, f32[2,128,24]{1,2,0:T(8,128)S(1)}, f32[2,128,24,128]{3,1,2,0:T(8,128)}, s32[256]{0:T(256)S(1)}, ...) while((s32[]{:T(128)}, f32[2,128,24]{1,2,0:T(8,128)S(1)}, ...), condition=%wide.region_10.10_spmd.clone, body=%wide.region_7.9_spmd.clone.sunk | while | flops 411381760 | bytes 42130116 | solution.py:58
  98.3 2.0 fusion.85
  100.2 1.3 fusion.87
  101.8 1.4 bitcast_dynamic-update-slice_fusion.6
  103.2 1.7 copy-done.5
  105.0 2.0 fusion.85
  107.0 1.3 fusion.87
  108.5 1.4 bitcast_dynamic-update-slice_fusion.6
  109.9 1.7 copy-done.5
  111.6 2.4 %divide_convert_fusion = bf16[2,128,24,128]{3,1,2,0:T(8,128)(2,1)S(1)} fusion(f32[2,128,24,128]{3,1,2,0:T(8,128)} %get-tuple-element.295, f32[2,128,24]{1,2,0:T(8,128)S(1)} %get-tuple-element.296), kind=kLoop, calls=%fused_computation.79 | loop fusion | flops 1572864 | bytes 4743168 | tf_op jit(solution)/shard_map/convert_element_type | solution.py:73
  114.0 1.0 copy.17
  115.0 18.4 %convolution_convert_fusion = bf16[256,6144]{1,0:T(8,128)(2,1)} fusion(bf16[3072,6144]{1,0:T(8,128)(2,1)} %param.22, bf16[32,8,24,128]{3,2,1,0:T(8,128)(2,1)S(1)} %bitcast.117), kind=kOutput, calls=%fused_computation.68 | convolution fusion | flops 9665249280 | bytes 42467328 | tf_op jit(solution)/shard_map/dot_general | solution.py:74
  133.4 0.7 copy-done.11
  134.1 80.4 %all-reduce.2.cloned.1.call-done = bf16[256,6144]{1,0:T(8,128)(2,1)} async-done(((bf16[256,6144]{1,0:T(8,128)(2,1)}), bf16[256,6144]{1,0:T(8,128)(2,1)}) %all-reduce.2.cloned.1.call-update) | async-done | bytes 3145744 | tf_op jit(solution)/shard_map/psum | solution.py:75
  214.5 5.7 %fusion.50 = bf16[256,6144]{1,0:T(8,128)(2,1)} fusion(bf16[256,6144]{1,0:T(8,128)(2,1)} %param.16, bf16[256,6144]{1,0:T(8,128)(2,1)} %all-reduce.2.cloned.1.call-done, f32[6144]{0:T(1024)S(1)} %convert_element_type.62), kind=kLoop, calls=%fused_computation.76 | loop fusion | flops 7864320 | bytes 9461760 | tf_op jit(solution)/shard_map/convert_element_type | solution.py:76
  (100 shorter events, 2.0 us)
Async XLA Ops:
  7.2 28.2 %copy-start = (bf16[6144,256]{1,0:T(8,128)(2,1)S(1)}, bf16[6144,256]{1,0:T(8,128)(2,1)}, u32[]{:S(2)}) copy-start(bf16[6144,256]{1,0:T(8,128)(2,1)} %param.20) | copy-start | bytes 9437188
  7.2 207.3 %all-reduce.2.cloned.1.call-start = ((), (), s32[]{:S(2)}) async-start(), calls=%async_computation | async-start | bytes 6291456 | tf_op jit(solution)/shard_map/psum | solution.py:75
  7.3 5.0 %copy-start.6 = (bf16[256,6144]{1,0:T(8,128)(2,1)S(1)}, bf16[256,6144]{1,0:T(8,128)(2,1)}, u32[]{:S(2)}) copy-start(bf16[256,6144]{1,0:T(8,128)(2,1)} %param.16) | copy-start | bytes 9437188
  9.8 3.4 %copy-start.9 = (s32[256]{0:T(256)S(1)}, s32[256]{0:T(256)}, u32[]{:S(2)}) copy-start(s32[256]{0:T(256)} %param.17) | copy-start | bytes 3076
  9.8 3.4 %copy-start.12 = (bf16[3072]{0:T(1024)(128)(2,1)S(1)}, bf16[3072]{0:T(1024)(128)(2,1)}, u32[]{:S(2)}) copy-start(bf16[3072]{0:T(1024)(128)(2,1)} %param.19) | copy-start | bytes 18436
  32.0 3.4 %copy-start.7 = (bf16[256,6144]{1,0:T(8,128)(2,1)S(1)}, bf16[256,6144]{1,0:T(8,128)(2,1)}, u32[]{:S(2)}) copy-start(bf16[256,6144]{1,0:T(8,128)(2,1)} %param.16) | copy-start | bytes 9437188
  37.0 3.4 %copy-start.2 = (f32[2,128,24,128]{3,1,2,0:T(8,128)S(1)}, f32[2,128,24,128]{3,1,2,0:T(8,128)}, u32[]{:S(2)}) copy-start(f32[2,128,24,128]{3,1,2,0:T(8,128)} %get-tuple-element.740) | copy-start | bytes 9437188 | tf_op jit(solution)/shard_map/while
  41.7 1.7 copy-start.3
  43.5 3.4 %copy-start.2 = (f32[2,128,24,128]{3,1,2,0:T(8,128)S(1)}, f32[2,128,24,128]{3,1,2,0:T(8,128)}, u32[]{:S(2)}) copy-start(f32[2,128,24,128]{3,1,2,0:T(8,128)} %get-tuple-element.740) | copy-start | bytes 9437188 | tf_op jit(solution)/shard_map/while
  48.3 1.7 copy-start.3
  49.9 0.6 copy-start.8
  49.9 0.6 copy-start.10
  50.6 6.8 %collective-permute-start = (bf16[256,256]{1,0:T(8,128)(2,1)S(1)}, bf16[256,256]{1,0:T(8,128)(2,1)S(1)}, u32[]{:S(2)}, u32[]{:S(2)}) collective-permute-start(bf16[256,256]{1,0:T(8,128)(2,1)S(1)} %get-tuple-element.772), channel_id=1, source_target_pairs={{0,1},{1,2},{2,3},{4,5},{5,6},{6,7}} | collective-permute-start | bytes 393224 | tf_op jit(solution)/shard_map/while/body/eval_jaxpr/ppermute | solution.py:67
  52.5 4.9 %collective-permute-start.1 = (s32[256]{0:T(256)S(1)}, s32[256]{0:T(256)S(1)}, u32[]{:S(2)}, u32[]{:S(2)}) collective-permute-start(s32[256]{0:T(256)S(1)} %get-tuple-element.773), channel_id=1, source_target_pairs={{0,1},{1,2},{2,3},{4,5},{5,6},{6,7}} | collective-permute-start | bytes 3080 | tf_op jit(solution)/shard_map/while/body/eval_jaxpr/ppermute | solution.py:68
  57.6 3.4 %copy-start.4 = (f32[2,128,24,128]{3,1,2,0:T(8,128)S(1)}, f32[2,128,24,128]{3,1,2,0:T(8,128)}, u32[]{:S(2)}) copy-start(f32[2,128,24,128]{3,1,2,0:T(8,128)} %get-tuple-element.707) | copy-start | bytes 9437188 | tf_op jit(solution)/shard_map/while/body/eval_jaxpr/while
  62.5 1.7 copy-start.5
  64.3 3.4 %copy-start.4 = (f32[2,128,24,128]{3,1,2,0:T(8,128)S(1)}, f32[2,128,24,128]{3,1,2,0:T(8,128)}, u32[]{:S(2)}) copy-start(f32[2,128,24,128]{3,1,2,0:T(8,128)} %get-tuple-element.707) | copy-start | bytes 9437188 | tf_op jit(solution)/shard_map/while/body/eval_jaxpr/while
  69.2 1.7 copy-start.5
  70.9 6.8 %collective-permute-start = (bf16[256,256]{1,0:T(8,128)(2,1)S(1)}, bf16[256,256]{1,0:T(8,128)(2,1)S(1)}, u32[]{:S(2)}, u32[]{:S(2)}) collective-permute-start(bf16[256,256]{1,0:T(8,128)(2,1)S(1)} %get-tuple-element.772), channel_id=1, source_target_pairs={{0,1},{1,2},{2,3},{4,5},{5,6},{6,7}} | collective-permute-start | bytes 393224 | tf_op jit(solution)/shard_map/while/body/eval_jaxpr/ppermute | solution.py:67
  72.8 4.9 %collective-permute-start.1 = (s32[256]{0:T(256)S(1)}, s32[256]{0:T(256)S(1)}, u32[]{:S(2)}, u32[]{:S(2)}) collective-permute-start(s32[256]{0:T(256)S(1)} %get-tuple-element.773), channel_id=1, source_target_pairs={{0,1},{1,2},{2,3},{4,5},{5,6},{6,7}} | collective-permute-start | bytes 3080 | tf_op jit(solution)/shard_map/while/body/eval_jaxpr/ppermute | solution.py:68
  77.9 3.4 %copy-start.4 = (f32[2,128,24,128]{3,1,2,0:T(8,128)S(1)}, f32[2,128,24,128]{3,1,2,0:T(8,128)}, u32[]{:S(2)}) copy-start(f32[2,128,24,128]{3,1,2,0:T(8,128)} %get-tuple-element.707) | copy-start | bytes 9437188 | tf_op jit(solution)/shard_map/while/body/eval_jaxpr/while
  82.8 1.7 copy-start.5
  84.6 3.4 %copy-start.4 = (f32[2,128,24,128]{3,1,2,0:T(8,128)S(1)}, f32[2,128,24,128]{3,1,2,0:T(8,128)}, u32[]{:S(2)}) copy-start(f32[2,128,24,128]{3,1,2,0:T(8,128)} %get-tuple-element.707) | copy-start | bytes 9437188 | tf_op jit(solution)/shard_map/while/body/eval_jaxpr/while
  89.6 1.7 copy-start.5
  91.3 6.8 %collective-permute-start = (bf16[256,256]{1,0:T(8,128)(2,1)S(1)}, bf16[256,256]{1,0:T(8,128)(2,1)S(1)}, u32[]{:S(2)}, u32[]{:S(2)}) collective-permute-start(bf16[256,256]{1,0:T(8,128)(2,1)S(1)} %get-tuple-element.772), channel_id=1, source_target_pairs={{0,1},{1,2},{2,3},{4,5},{5,6},{6,7}} | collective-permute-start | bytes 393224 | tf_op jit(solution)/shard_map/while/body/eval_jaxpr/ppermute | solution.py:67
  93.2 4.9 %collective-permute-start.1 = (s32[256]{0:T(256)S(1)}, s32[256]{0:T(256)S(1)}, u32[]{:S(2)}, u32[]{:S(2)}) collective-permute-start(s32[256]{0:T(256)S(1)} %get-tuple-element.773), channel_id=1, source_target_pairs={{0,1},{1,2},{2,3},{4,5},{5,6},{6,7}} | collective-permute-start | bytes 3080 | tf_op jit(solution)/shard_map/while/body/eval_jaxpr/ppermute | solution.py:68
  98.2 3.4 %copy-start.4 = (f32[2,128,24,128]{3,1,2,0:T(8,128)S(1)}, f32[2,128,24,128]{3,1,2,0:T(8,128)}, u32[]{:S(2)}) copy-start(f32[2,128,24,128]{3,1,2,0:T(8,128)} %get-tuple-element.707) | copy-start | bytes 9437188 | tf_op jit(solution)/shard_map/while/body/eval_jaxpr/while
  103.2 1.7 copy-start.5
  105.0 3.4 %copy-start.4 = (f32[2,128,24,128]{3,1,2,0:T(8,128)S(1)}, f32[2,128,24,128]{3,1,2,0:T(8,128)}, u32[]{:S(2)}) copy-start(f32[2,128,24,128]{3,1,2,0:T(8,128)} %get-tuple-element.707) | copy-start | bytes 9437188 | tf_op jit(solution)/shard_map/while/body/eval_jaxpr/while
  109.9 1.7 copy-start.5
  133.4 0.7 copy-start.11
  134.1 86.0 %copy-start.1 = (bf16[6144,256]{1,0:T(8,128)(2,1)S(1)}, bf16[6144,256]{1,0:T(8,128)(2,1)}, u32[]{:S(2)}) copy-start(bf16[6144,256]{1,0:T(8,128)(2,1)} %param.20) | copy-start | bytes 9437188
Sparse Core Ops, SparseCore 0:
  133.6 80.8 all-reduce.1
where the time goes:
time: 229 us; the launch traced here: 227 us
  waiting for transfers between devices  89.3 us (39%)
  matrix products  65.5 us (29%)
  other arithmetic  25.6 us (11%)
  local copies, waits for them, and re-layouts  20.1 us (9%)
  between operations  14.2 us (6%)
  starting transfers between devices  11.5 us (5%)
    psum x1, waiting for transfers between devices, local_block(): proj_sum = lax.psum(partial, 'tp')  80.4 us
    dot_general x1, matrix products, local_block(): jnp.dot(normed, w_q, preferred_element_type=jnp.float32)  18.7 us
    dot_general x1, matrix products, local_block(): jnp.dot(attn_out, w_o, preferred_element_type=jnp.float32)  18.4 us
    dot_general x8, matrix products, merge_block(): jnp.einsum('bhd,kd->bhk', q_blk, k_blk, preferred_element_type=jnp.float32)  15.8 us
    while x38, local copies, waits for them, and re-layouts  13.4 us
    dot_general x8, matrix products, merge_block(): jnp.einsum('bhk,kd->bhd', p_weights, v_float, preferred_element_type=jnp....  11.2 us
    reduce_sum x8, other arithmetic, merge_block(): l_new = l_prev * rescale + jnp.sum(p_weights, axis=-1)  10.6 us
    ppermute x3, waiting for transfers between devices, shift_step(): seg_keys = lax.ppermute(seg_keys, 'cp', send_pairs)  8.88 us
  transfers between devices with their start and end apart: 7, of which 4 were waited for; matrix products, arithmetic and copies ran while one was open for 0% of the time, Pallas kernels for 0%

commit v1 on v0

v1 whole, which is shorter than its diff:
```python
import functools

import jax
import jax.numpy as jnp
from jax import lax
from jax.experimental import pallas as pl
from jax.experimental.pallas import tpu as pltpu
from jax.sharding import PartitionSpec as P

HEAD_DIM = 128
LN_EPS = 1e-5
EXP2_SCALE = HEAD_DIM ** -0.5 * 1.4426950408889634
MESH = pl.DeviceIdType.MESH

ROWS = 128
TILE_K = 3072
TILE_N = 512
SLOTS = 11
LN_ROWS = 32


def block_kernel(n_cp, hid_hbm, seg_ref, wq_hbm, bq_ref, wkv_hbm, bkv_ref, wo_hbm, bo_ref, gain_ref, bias_ref,
                 y_ref, k_ref, v_ref,
                 normed, wkv, wbuf, kv_all, seg_all, mask, qbuf, obuf, send, recv,
                 hid_sem, wkv_sem, w_sem, kv_send, kv_recv, seg_send, seg_recv, tp_send, tp_recv):
    my = lax.axis_index('cp')
    partner = 1 - lax.axis_index('tp')
    tok, d_model = y_ref.shape
    q_width = qbuf.shape[1]
    n_chunk = tok // ROWS
    q_tiles = q_width // TILE_N
    k_halves = d_model // TILE_K
    o_tiles = d_model // TILE_N
    q_items = q_tiles * k_halves
    items = q_items + o_tiles
    total = n_chunk * items

    barrier = pltpu.get_barrier_semaphore()
    for step in range(1, n_cp):
        pl.semaphore_signal(barrier, inc=1, device_id={'cp': lax.rem(my + step, n_cp)}, device_id_type=MESH)
    pl.semaphore_signal(barrier, inc=1, device_id={'tp': partner}, device_id_type=MESH)

    def hid_copy(i):
        rows = pl.ds(i * LN_ROWS, LN_ROWS)
        return pltpu.make_async_copy(hid_hbm.at[rows, :], y_ref.at[rows, :], hid_sem.at[i])

    def w_issue(g):
        slot = lax.rem(g, SLOTS)
        item = lax.rem(g, items)

        @pl.when(item < q_items)
        def _():
            col = pl.multiple_of(lax.div(item, k_halves) * TILE_N, TILE_N)
            row = pl.multiple_of(lax.rem(item, k_halves) * TILE_K, TILE_K)
            pltpu.make_async_copy(wq_hbm.at[pl.ds(row, TILE_K), pl.ds(col, TILE_N)], wbuf.at[slot], w_sem.at[slot]).start()

        @pl.when(item >= q_items)
        def _():
            col = pl.multiple_of((item - q_items) * TILE_N, TILE_N)
            pltpu.make_async_copy(wo_hbm.at[:, pl.ds(col, TILE_N)], wbuf.at[slot], w_sem.at[slot]).start()

    def w_wait(g):
        slot = lax.rem(g, SLOTS)
        pltpu.make_async_copy(wo_hbm.at[:, pl.ds(0, TILE_N)], wbuf.at[slot], w_sem.at[slot]).wait()
        return slot

    def w_next(g):
        @pl.when(g + SLOTS < total)
        def _():
            w_issue(g + SLOTS)

    n_ln = tok // LN_ROWS
    for i in range(n_ln):
        hid_copy(i).start()
    wkv_copy = pltpu.make_async_copy(wkv_hbm, wkv, wkv_sem)
    wkv_copy.start()
    for g in range(SLOTS - n_ln):
        w_issue(jnp.int32(g))

    def ln_block(i, carry):
        hid_copy(i).wait()
        w_issue(i + SLOTS - n_ln)
        rows = pl.ds(pl.multiple_of(i * LN_ROWS, LN_ROWS), LN_ROWS)
        n_col = d_model // 128

        def load(j):
            return y_ref[rows, j * 128:(j + 1) * 128].astype(jnp.float32)

        accs = [load(j) for j in range(4)]
        for j in range(4, n_col):
            accs[j % 4] = accs[j % 4] + load(j)
        mean = jnp.sum((accs[0] + accs[1]) + (accs[2] + accs[3]), axis=-1, keepdims=True) * (1.0 / d_model)
        mean = jnp.broadcast_to(mean, (LN_ROWS, 128))
        accs = [None] * 4
        for j in range(n_col):
            cen = load(j) - mean
            accs[j % 4] = cen * cen if accs[j % 4] is None else accs[j % 4] + cen * cen
        var = jnp.sum((accs[0] + accs[1]) + (accs[2] + accs[3]), axis=-1, keepdims=True) * (1.0 / d_model)
        rstd = jnp.broadcast_to(lax.rsqrt(var + LN_EPS), (LN_ROWS, 128))
        for j in range(n_col):
            cols = slice(j * 128, (j + 1) * 128)
            out = (load(j) - mean) * rstd * gain_ref[:, cols].astype(jnp.float32) + bias_ref[:, cols].astype(jnp.float32)
            normed[rows, cols] = out.astype(jnp.bfloat16)
        return carry

    lax.fori_loop(0, n_ln, ln_block, 0)

    wkv_copy.wait()
    kv_own = jnp.dot(normed[...], wkv[...], preferred_element_type=jnp.float32) + bkv_ref[...].astype(jnp.float32)
    kv_own = kv_own.astype(jnp.bfloat16)
    kv_all[pl.ds(my, 1)] = kv_own[None]
    seg_all[pl.ds(my, 1)] = seg_ref[...][None]
    k_ref[...] = kv_own[:, :HEAD_DIM]
    v_ref[...] = kv_own[:, HEAD_DIM:]

    pl.semaphore_wait(barrier, n_cp)

    def kv_copies(src, dst):
        return (pltpu.make_async_remote_copy(src_ref=kv_all.at[src], dst_ref=kv_all.at[src], send_sem=kv_send.at[dst],
                                             recv_sem=kv_recv.at[src], device_id={'cp': dst}, device_id_type=MESH),
                pltpu.make_async_remote_copy(src_ref=seg_ref, dst_ref=seg_all.at[src], send_sem=seg_send.at[dst],
                                             recv_sem=seg_recv.at[src], device_id={'cp': dst}, device_id_type=MESH))

    for dst in range(1, n_cp):
        @pl.when(my < dst)
        def _():
            for copy in kv_copies(my, dst):
                copy.start()

    def tile_copy(t):
        return pltpu.make_async_remote_copy(src_ref=send.at[t], dst_ref=recv.at[t], send_sem=tp_send.at[t],
                                            recv_sem=tp_recv.at[t], device_id={'tp': partner}, device_id_type=MESH)

    def chunk(c, carry):
        base = c * items
        rows = pl.ds(pl.multiple_of(c * ROWS, ROWS), ROWS)

        def q_tile(j, carry):
            acc = None
            for half in range(k_halves):
                g = base + j * k_halves + half
                slot = w_wait(g)
                part = jnp.dot(normed[rows, half * TILE_K:(half + 1) * TILE_K], wbuf[slot], preferred_element_type=jnp.float32)
                acc = part if acc is None else acc + part
                w_next(g)
            cols = pl.ds(pl.multiple_of(j * TILE_N, TILE_N), TILE_N)
            qbuf[:, cols] = (acc + bq_ref[:, cols].astype(jnp.float32)).astype(jnp.bfloat16)
            return carry

        lax.fori_loop(0, q_tiles, q_tile, 0)

        @pl.when(c == 0)
        def _():
            for src in range(n_cp - 1):
                @pl.when(src < my)
                def _():
                    for copy in kv_copies(src, src):
                        copy.wait_recv()

        seg_q = jnp.broadcast_to(seg_ref[pl.ds(c, 1), :].astype(jnp.float32), (ROWS, ROWS)).T
        q_pos = my * tok + c * ROWS + lax.broadcasted_iota(jnp.int32, (ROWS, 128), 0)
        lane = lax.broadcasted_iota(jnp.int32, (ROWS, 128), 1)
        for b in range(n_cp * tok // 128):
            src, part = b * 128 // tok, b % (tok // 128)

            @pl.when(src <= my)
            def _():
                seg_k = seg_all[src, part:part + 1, :].astype(jnp.float32)
                seen = (seg_q == seg_k) & (lane + b * 128 <= q_pos)
                mask[:, b * 128:(b + 1) * 128] = jnp.where(seen, 0.0, -jnp.inf)

        def head_pair(p, carry):
            q_two = qbuf[:, pl.ds(pl.multiple_of(p * 256, 256), 256)]
            q_rows = jnp.concatenate([q_two[:, :HEAD_DIM], q_two[:, HEAD_DIM:]], axis=0)
            for nb in range(1, n_cp + 1):
                @pl.when(my == nb - 1)
                def _():
                    keys = nb * tok
                    k_blk = kv_all[0:nb, :, :HEAD_DIM].reshape(keys, HEAD_DIM)
                    v_blk = kv_all[0:nb, :, HEAD_DIM:].reshape(keys, HEAD_DIM)
                    s = lax.dot_general(q_rows, k_blk, (((1,), (1,)), ((), ())), preferred_element_type=jnp.float32)
                    s = s.reshape(2, ROWS, keys) + mask[:, :keys][None]
                    p_wts = jnp.exp2((s - jnp.max(s, axis=-1, keepdims=True)) * EXP2_SCALE)
                    l_sum = jnp.sum(p_wts, axis=-1, keepdims=True).reshape(2 * ROWS, 1)
                    o = jnp.dot(p_wts.reshape(2 * ROWS, keys).astype(jnp.bfloat16), v_blk, preferred_element_type=jnp.float32)
                    o = (o / l_sum).astype(jnp.bfloat16)
                    obuf[:, pl.ds(pl.multiple_of(p * 256, 256), 256)] = jnp.concatenate([o[:ROWS], o[ROWS:]], axis=1)
            return carry

        lax.fori_loop(0, q_width // 256, head_pair, 0)

        def o_tile(n, carry):
            g = base + q_items + n
            slot = w_wait(g)
            t = c * o_tiles + n
            send[t] = jnp.dot(obuf[...], wbuf[slot], preferred_element_type=jnp.float32).astype(jnp.bfloat16)
            tile_copy(t).start()
            w_next(g)
            return carry

        lax.fori_loop(0, o_tiles, o_tile, 0)
        return carry

    lax.fori_loop(0, n_chunk, chunk, 0)

    for dst in range(1, n_cp):
        @pl.when(my < dst)
        def _():
            for copy in kv_copies(my, dst):
                copy.wait_send()

    def finish(t, carry):
        copy = tile_copy(t)
        copy.wait_recv()
        copy.wait_send()
        rows = pl.ds(pl.multiple_of(lax.div(t, o_tiles) * ROWS, ROWS), ROWS)
        cols = pl.ds(pl.multiple_of(lax.rem(t, o_tiles) * TILE_N, TILE_N), TILE_N)
        both = send[t].astype(jnp.float32) + recv[t].astype(jnp.float32)
        y_ref[rows, cols] = (y_ref[rows, cols].astype(jnp.float32) + both + bo_ref[:, cols].astype(jnp.float32)).astype(jnp.bfloat16)
        return carry

    lax.fori_loop(0, n_chunk * o_tiles, finish, 0)


def solution(mesh):
    n_cp = mesh.shape['cp']

    def local_block(hidden, seg_ids, w_q, b_q, w_kv, b_kv, w_o, b_o, ln_gain, ln_bias):
        tok, d_model = hidden.shape
        q_width = w_q.shape[1]
        n_tiles = (tok // ROWS) * (d_model // TILE_N)
        vmem = pl.BlockSpec(memory_space=pltpu.VMEM)
        hbm = pl.BlockSpec(memory_space=pl.ANY)
        bf16, f32 = jnp.bfloat16, jnp.float32
        dma = pltpu.SemaphoreType.DMA
        flops = 2 * tok * d_model * (2 * q_width + 256)
        y, k, v = pl.pallas_call(
            functools.partial(block_kernel, n_cp),
            out_shape=(jax.ShapeDtypeStruct((tok, d_model), bf16),
                       jax.ShapeDtypeStruct((tok, HEAD_DIM), bf16),
                       jax.ShapeDtypeStruct((tok, HEAD_DIM), bf16)),
            in_specs=[hbm, vmem, hbm, vmem, hbm, vmem, hbm, vmem, vmem, vmem],
            out_specs=(vmem, vmem, vmem),
            scratch_shapes=[
                pltpu.VMEM((tok, d_model), bf16),
                pltpu.VMEM((d_model, 2 * HEAD_DIM), bf16),
                pltpu.VMEM((SLOTS, TILE_K, TILE_N), bf16),
                pltpu.VMEM((n_cp, tok, 2 * HEAD_DIM), bf16),
                pltpu.VMEM((n_cp, tok // 128, 128), jnp.int32),
                pltpu.VMEM((ROWS, n_cp * tok), f32),
                pltpu.VMEM((ROWS, q_width), bf16),
                pltpu.VMEM((ROWS, q_width), bf16),
                pltpu.VMEM((n_tiles, ROWS, TILE_N), bf16),
                pltpu.VMEM((n_tiles, ROWS, TILE_N), bf16),
                dma((tok // LN_ROWS,)), dma, dma((SLOTS,)),
                dma((n_cp,)), dma((n_cp,)), dma((n_cp,)), dma((n_cp,)),
                dma((n_tiles,)), dma((n_tiles,)),
            ],
            compiler_params=pltpu.CompilerParams(collective_id=0, has_side_effects=True, vmem_limit_bytes=62 * 1024 * 1024),
            cost_estimate=pl.CostEstimate(flops=flops, bytes_accessed=2 * 4 * d_model * q_width, transcendentals=0),
        )(hidden, seg_ids.reshape(tok // 128, 128), w_q, b_q.reshape(1, -1), w_kv, b_kv.reshape(1, -1), w_o,
          b_o.reshape(1, -1), ln_gain.reshape(1, -1), ln_bias.reshape(1, -1))
        return y, k, v

    row_spec = P(('dp', 'cp'), None)
    tok_spec = P(('dp', 'cp'))
    return jax.shard_map(local_block, mesh=mesh,
                         in_specs=(row_spec, tok_spec, P(None, 'tp'), P('tp'), P(None, None), P(None), P('tp', None), P(None), P(None), P(None)),
                         out_specs=(row_spec, row_spec, row_spec), check_vma=False)
```

time: 229 us -> 110 us (0.48)
  Pallas kernels: 0 us -> 96.9 us
  waiting for transfers between devices: 89.3 us -> 0 us
  matrix products: 65.5 us -> 0 us
  other arithmetic: 25.6 us -> 0 us
  between operations: 14.2 us -> 0.66 us
  starting transfers between devices: 11.5 us -> 0 us
  local copies, waits for them, and re-layouts: 20.1 us -> 11.7 us
    pallas_call x0 -> x1, Pallas kernels: none -> 96.9 us  [local_block(): pl.pallas_call(functools.partial(block_kernel, n_cp), out_shape=(jax.Shap...]
    psum x1 -> x0, waiting for transfers between devices: 80.4 us -> none  [local_block(): proj_sum = lax.psum(partial, 'tp')]
    dot_general x19 -> x0, matrix products: 65.5 us -> none  [the longest x1 18.7 us: local_block(): jnp.dot(normed, w_q, preferred_element_type=jnp.float32)]
    reduce_sum x10 -> x0, other arithmetic: 14 us -> none  [the longest x8 10.6 us: merge_block(): l_new = l_prev * rescale + jnp.sum(p_weights, axis=-1)]
    while x38 -> x0, local copies, waits for them, and re-layouts: 13.4 us -> none
    ppermute x6 -> x0, starting transfers between devices: 11.5 us -> none  [the longest x3 5.76 us: shift_step(): seg_keys = lax.ppermute(seg_keys, 'cp', send_pairs)]
    convert_element_type x7 -> x0, other arithmetic: 10.6 us -> none  [the longest x1 5.68 us: local_block(): (hidden.astype(jnp.float32) + proj_sum.astype(jnp.float32) + b_o.astype(j...]
    ppermute x6 -> x0, waiting for transfers between devices: 8.89 us -> none  [the longest x3 8.88 us: shift_step(): seg_keys = lax.ppermute(seg_keys, 'cp', send_pairs)]
  transfers between devices with their start and end apart: 7 -> 0, of which waited for: 4 -> 0; matrix products, arithmetic and copies ran while one was open for 0% -> 0% of each run, Pallas kernels for 0% -> 0%
where the time goes in v1:
time: 110 us; the launch traced here: 109 us
  Pallas kernels  96.9 us (88%)
  local copies, waits for them, and re-layouts  11.7 us (11%)
    pallas_call x1, Pallas kernels, local_block(): pl.pallas_call(functools.partial(block_kernel, n_cp), out_shape=(jax.Shap...  96.9 us
    unnamed x7, local copies, waits for them, and re-layouts  5.18 us

profile of v1, /device:TPU:2, one launch (start us, length us, event | category | flops | bytes accessed | tf_op | source)
XLA Modules:
  0.0 109.2 jit_solution(4498811376435457134)
XLA Ops:
  0.6 1.2 %reshape.26.bkv_ref = bf16[1,256]{1,0:T(2,128)(2,1)} reshape(bf16[256]{0:T(256)(128)(2,1)} %param.15) | data formatting | bytes 1024 | tf_op jit(solution)/shard_map/reshape | solution.py:261
  1.9 1.3 %reshape.25.bq_ref = bf16[1,3072]{1,0:T(2,128)(2,1)} reshape(bf16[3072]{0:T(1024)(128)(2,1)} %param.13) | data formatting | bytes 12288 | tf_op jit(solution)/shard_map/reshape | solution.py:261
  3.2 1.3 %reshape.27.bo_ref = bf16[1,6144]{1,0:T(2,128)(2,1)} reshape(bf16[6144]{0:T(1024)(128)(2,1)} %param.17) | data formatting | bytes 24576 | tf_op jit(solution)/shard_map/reshape | solution.py:262
  4.5 1.3 %reshape.28.gain_ref = bf16[1,6144]{1,0:T(2,128)(2,1)} reshape(bf16[6144]{0:T(1024)(128)(2,1)} %param.18) | data formatting | bytes 24576 | tf_op jit(solution)/shard_map/reshape | solution.py:262
  5.8 1.3 %reshape.29.bias_ref = bf16[1,6144]{1,0:T(2,128)(2,1)} reshape(bf16[6144]{0:T(1024)(128)(2,1)} %param.19) | data formatting | bytes 24576 | tf_op jit(solution)/shard_map/reshape | solution.py:262
  7.1 96.9 %shard_map.121 = (bf16[256,6144]{1,0:T(8,128)(2,1)}, bf16[256,128]{1,0:T(8,128)(2,1)}, bf16[256,128]{1,0:T(8,128)(2,1)}) custom-call(bf16[256,6144]{1,0:T(8,128)(2,1)} %hid_hbm.1, s32[2,128]{1,0:T(2,128)} %bitcast.1, bf16[6144,3072]{1,0:T(8,128)(2,1)} %wq_hbm.1, bf16[1,3072]{1,0:T(2,128)(2,1)} %reshape.25.bq_ref, bf16[6144,256]{1,0:T(8,128)(2,1)} %wkv_hbm.1, ...), custom_call_target="tpu_custom_call" | custom-call | flops 20132659200 | bytes 150994944 | tf_op jit(solution)/shard_map/pallas_call | solution.py:237
  104.0 0.0 copy-start.1
  104.0 0.0 copy-start
  104.0 3.9 %copy.16 = bf16[256,6144]{1,0:T(8,128)(2,1)} copy(bf16[256,6144]{1,0:T(8,128)(2,1)} %get-tuple-element.6) | data formatting | bytes 6291456
  107.9 0.0 copy-done.1
  107.9 0.6 copy.17
  108.6 0.0 copy-done
  108.6 0.6 copy.18
Async XLA Ops:
  104.0 3.9 %copy-start.1 = (bf16[256,128]{1,0:T(8,128)(2,1)S(1)}, bf16[256,128]{1,0:T(8,128)(2,1)}, u32[]{:S(2)}) copy-start(bf16[256,128]{1,0:T(8,128)(2,1)} %get-tuple-element.7) | copy-start | bytes 196612
  104.0 4.6 %copy-start = (bf16[256,128]{1,0:T(8,128)(2,1)S(1)}, bf16[256,128]{1,0:T(8,128)(2,1)}, u32[]{:S(2)}) copy-start(bf16[256,128]{1,0:T(8,128)(2,1)} %get-tuple-element.8) | copy-start | bytes 196612

commit v2 on v1

v2 whole, which is shorter than its diff:
```python
import functools

import jax
import jax.numpy as jnp
from jax import lax
from jax.experimental import pallas as pl
from jax.experimental.pallas import tpu as pltpu
from jax.sharding import PartitionSpec as P

HEAD_DIM = 128
LN_EPS = 1e-5
EXP2_SCALE = HEAD_DIM ** -0.5 * 1.4426950408889634
MESH = pl.DeviceIdType.MESH

ROWS = 128
TILE_K = 3072
TILE_N = 512
SLOTS = 10
LAG = 3
LN_ROWS = 32


def block_kernel(n_cp, hid_hbm, seg_hbm, wq_hbm, bq_hbm, wkv_hbm, bkv_hbm, wo_hbm, bo_hbm, gain_hbm, bias_hbm,
                 y_ref, k_ref, v_ref,
                 normed, wkv, wbuf, kv_all, seg_all, mask, qbuf, obuf, send, recv,
                 bq_raw, bkv_raw, bo_raw, gain_raw, bias_raw, bq, bkv, bo, gain, bias,
                 hid_sem, wkv_sem, small_sem, w_sem, kv_send, kv_recv, seg_send, seg_recv, tp_send, tp_recv):
    my = lax.axis_index('cp')
    partner = 1 - lax.axis_index('tp')
    tok, d_model = y_ref.shape
    q_width = qbuf.shape[1]
    n_chunk = tok // ROWS
    q_tiles = q_width // TILE_N
    k_halves = d_model // TILE_K
    o_tiles = d_model // TILE_N
    q_items = q_tiles * k_halves
    items = q_items + o_tiles
    total = n_chunk * items
    f32, bf16 = jnp.float32, jnp.bfloat16

    def hid_copy(i):
        rows = pl.ds(i * LN_ROWS, LN_ROWS)
        return pltpu.make_async_copy(hid_hbm.at[rows, :], y_ref.at[rows, :], hid_sem.at[i])

    def w_issue(g):
        slot = lax.rem(g, SLOTS)
        item = lax.rem(g, items)

        @pl.when(item < q_items)
        def _():
            col = pl.multiple_of(lax.div(item, k_halves) * TILE_N, TILE_N)
            row = pl.multiple_of(lax.rem(item, k_halves) * TILE_K, TILE_K)
            pltpu.make_async_copy(wq_hbm.at[pl.ds(row, TILE_K), pl.ds(col, TILE_N)], wbuf.at[slot], w_sem.at[slot]).start()

        @pl.when(item >= q_items)
        def _():
            col = pl.multiple_of((item - q_items) * TILE_N, TILE_N)
            pltpu.make_async_copy(wo_hbm.at[:, pl.ds(col, TILE_N)], wbuf.at[slot], w_sem.at[slot]).start()

    def w_wait(g):
        slot = lax.rem(g, SLOTS)
        pltpu.make_async_copy(wo_hbm.at[:, pl.ds(0, TILE_N)], wbuf.at[slot], w_sem.at[slot]).wait()
        return slot

    def w_next(g):
        @pl.when(g + SLOTS < total)
        def _():
            w_issue(g + SLOTS)

    n_ln = tok // LN_ROWS
    hid_copy(0).start()
    small = [pltpu.make_async_copy(src, dst, small_sem.at[i]) for i, (src, dst) in enumerate((
        (gain_hbm, gain_raw), (bias_hbm, bias_raw), (bkv_hbm, bkv_raw), (bq_hbm, bq_raw), (bo_hbm, bo_raw), (seg_hbm, seg_all.at[my])))]
    for copy in small:
        copy.start()
    for i in range(1, n_ln):
        hid_copy(i).start()
    wkv_copy = pltpu.make_async_copy(wkv_hbm, wkv, wkv_sem)
    wkv_copy.start()
    for g in range(SLOTS - n_ln):
        w_issue(jnp.int32(g))

    barrier = pltpu.get_barrier_semaphore()
    for step in range(1, n_cp):
        pl.semaphore_signal(barrier, inc=1, device_id={'cp': lax.rem(my + step, n_cp)}, device_id_type=MESH)
    pl.semaphore_signal(barrier, inc=1, device_id={'tp': partner}, device_id_type=MESH)

    for copy in small:
        copy.wait()
    gain[...] = gain_raw[...].astype(f32)
    bias[...] = bias_raw[...].astype(f32)
    bkv[...] = bkv_raw[...].astype(f32)
    bq[...] = bq_raw[...].astype(f32)
    bo[...] = bo_raw[...].astype(f32)

    def ln_block(i, carry):
        hid_copy(i).wait()
        w_issue(i + SLOTS - n_ln)
        rows = pl.ds(pl.multiple_of(i * LN_ROWS, LN_ROWS), LN_ROWS)
        n_col = d_model // 128

        def load(j):
            return y_ref[rows, j * 128:(j + 1) * 128].astype(f32)

        accs = [load(j) for j in range(4)]
        for j in range(4, n_col):
            accs[j % 4] = accs[j % 4] + load(j)
        mean = jnp.sum((accs[0] + accs[1]) + (accs[2] + accs[3]), axis=-1, keepdims=True) * (1.0 / d_model)
        mean = jnp.broadcast_to(mean, (LN_ROWS, 128))
        accs = [None] * 4
        for j in range(n_col):
            cen = load(j) - mean
            accs[j % 4] = cen * cen if accs[j % 4] is None else accs[j % 4] + cen * cen
        var = jnp.sum((accs[0] + accs[1]) + (accs[2] + accs[3]), axis=-1, keepdims=True) * (1.0 / d_model)
        rstd = jnp.broadcast_to(lax.rsqrt(var + LN_EPS), (LN_ROWS, 128))
        for j in range(n_col):
            out = (load(j) - mean) * rstd * gain[j:j + 1, :] + bias[j:j + 1, :]
            normed[rows, j * 128:(j + 1) * 128] = out.astype(bf16)
        return carry

    def kv_copy(src, h, dst):
        rows = pl.ds(pl.multiple_of(h * ROWS, ROWS), ROWS)
        return pltpu.make_async_remote_copy(src_ref=kv_all.at[src, rows, :], dst_ref=kv_all.at[src, rows, :],
                                            send_sem=kv_send.at[dst, h], recv_sem=kv_recv.at[src, h],
                                            device_id={'cp': dst}, device_id_type=MESH)

    def seg_copy(src, dst):
        return pltpu.make_async_remote_copy(src_ref=seg_all.at[src], dst_ref=seg_all.at[src], send_sem=seg_send.at[dst],
                                            recv_sem=seg_recv.at[src], device_id={'cp': dst}, device_id_type=MESH)

    ln_half = n_ln // n_chunk

    def kv_half(h, carry):
        lax.fori_loop(h * ln_half, (h + 1) * ln_half, ln_block, 0)
        rows = pl.ds(pl.multiple_of(h * ROWS, ROWS), ROWS)

        @pl.when(h == 0)
        def _():
            wkv_copy.wait()

        part = jnp.dot(normed[rows, :], wkv[...], preferred_element_type=f32)
        k_own = (part[:, :HEAD_DIM] + bkv[0:1, :]).astype(bf16)
        v_own = (part[:, HEAD_DIM:] + bkv[1:2, :]).astype(bf16)
        kv_all[pl.ds(my, 1), rows, :HEAD_DIM] = k_own[None]
        kv_all[pl.ds(my, 1), rows, HEAD_DIM:] = v_own[None]
        k_ref[rows, :] = k_own
        v_ref[rows, :] = v_own

        @pl.when(h == 0)
        def _():
            pl.semaphore_wait(barrier, n_cp)
            for dst in range(1, n_cp):
                @pl.when(my < dst)
                def _():
                    seg_copy(my, dst).start()

        for dst in range(1, n_cp):
            @pl.when(my < dst)
            def _():
                kv_copy(my, h, dst).start()
        return carry

    lax.fori_loop(0, n_chunk, kv_half, 0)

    def tile_copy(t):
        return pltpu.make_async_remote_copy(src_ref=send.at[t], dst_ref=recv.at[t], send_sem=tp_send.at[t],
                                            recv_sem=tp_recv.at[t], device_id={'tp': partner}, device_id_type=MESH)

    def chunk(c, carry):
        base = c * items
        rows = pl.ds(pl.multiple_of(c * ROWS, ROWS), ROWS)

        def q_tile(j):
            acc = None
            for half in range(k_halves):
                g = base + j * k_halves + half
                slot = w_wait(g)
                part = jnp.dot(normed[rows, half * TILE_K:(half + 1) * TILE_K], wbuf[slot], preferred_element_type=f32)
                acc = part if acc is None else acc + part
                w_next(g)
            for i in range(TILE_N // 128):
                cols = pl.ds(pl.multiple_of(j * TILE_N + i * 128, 128), 128)
                row = j * (TILE_N // 128) + i
                qbuf[:, cols] = (acc[:, i * 128:(i + 1) * 128] + bq[pl.ds(row, 1), :]).astype(bf16)

        def make_mask():
            @pl.when(c == 0)
            def _():
                for src in range(n_cp - 1):
                    @pl.when(src < my)
                    def _():
                        seg_copy(src, src).wait_recv()
                        for h in range(n_chunk):
                            kv_copy(src, h, src).wait_recv()

            seg_q = jnp.broadcast_to(seg_all[my, pl.ds(c, 1), :].astype(f32), (ROWS, ROWS)).T
            q_pos = my * tok + c * ROWS + lax.broadcasted_iota(jnp.int32, (ROWS, 128), 0)
            lane = lax.broadcasted_iota(jnp.int32, (ROWS, 128), 1)
            for b in range(n_cp * tok // 128):
                src, part = b * 128 // tok, b % (tok // 128)

                @pl.when(src <= my)
                def _():
                    seg_k = seg_all[src, part:part + 1, :].astype(f32)
                    seen = (seg_q == seg_k) & (lane + b * 128 <= q_pos)
                    mask[:, b * 128:(b + 1) * 128] = jnp.where(seen, 0.0, -jnp.inf)

        def head_pair(p, carry):
            q_two = qbuf[:, pl.ds(pl.multiple_of(p * 256, 256), 256)]
            q_rows = jnp.concatenate([q_two[:, :HEAD_DIM], q_two[:, HEAD_DIM:]], axis=0)
            for nb in range(1, n_cp * n_chunk + 1):
                @pl.when(my * n_chunk + c == nb - 1)
                def _():
                    keys = nb * ROWS
                    full = -(-keys // tok)
                    k_blk = kv_all[0:full, :, :HEAD_DIM].reshape(full * tok, HEAD_DIM)[:keys]
                    v_blk = kv_all[0:full, :, HEAD_DIM:].reshape(full * tok, HEAD_DIM)[:keys]
                    s = lax.dot_general(q_rows, k_blk, (((1,), (1,)), ((), ())), preferred_element_type=f32)
                    s = s.reshape(2, ROWS, keys) + mask[:, :keys][None]
                    p_wts = jnp.exp2((s - jnp.max(s, axis=-1, keepdims=True)) * EXP2_SCALE)
                    l_sum = jnp.sum(p_wts, axis=-1, keepdims=True).reshape(2 * ROWS, 1)
                    o = jnp.dot(p_wts.reshape(2 * ROWS, keys).astype(bf16), v_blk, preferred_element_type=f32)
                    o = (o / l_sum).astype(bf16)
                    obuf[:, pl.ds(pl.multiple_of(p * 256, 256), 256)] = jnp.concatenate([o[:ROWS], o[ROWS:]], axis=1)
            return carry

        pairs = TILE_N // 256

        def stage(u, carry):
            @pl.when(u < q_tiles)
            def _():
                q_tile(u)

            @pl.when(u == LAG)
            def _():
                make_mask()

            @pl.when(u >= LAG)
            def _():
                lax.fori_loop((u - LAG) * pairs, (u - LAG + 1) * pairs, head_pair, 0)
            return carry

        lax.fori_loop(0, q_tiles + LAG, stage, 0)

        def o_tile(n, carry):
            g = base + q_items + n
            slot = w_wait(g)
            t = c * o_tiles + n
            send[t] = jnp.dot(obuf[...], wbuf[slot], preferred_element_type=f32).astype(bf16)
            tile_copy(t).start()
            w_next(g)
            return carry

        lax.fori_loop(0, o_tiles, o_tile, 0)
        return carry

    lax.fori_loop(0, n_chunk, chunk, 0)

    for dst in range(1, n_cp):
        @pl.when(my < dst)
        def _():
            seg_copy(my, dst).wait_send()
            for h in range(n_chunk):
                kv_copy(my, h, dst).wait_send()

    def finish(t, carry):
        copy = tile_copy(t)
        copy.wait_recv()
        copy.wait_send()
        n = lax.rem(t, o_tiles)
        rows = pl.ds(pl.multiple_of(lax.div(t, o_tiles) * ROWS, ROWS), ROWS)
        for i in range(TILE_N // 128):
            cols = pl.ds(pl.multiple_of(n * TILE_N + i * 128, 128), 128)
            part = slice(i * 128, (i + 1) * 128)
            both = send[t, :, part].astype(f32) + recv[t, :, part].astype(f32)
            y_ref[rows, cols] = (y_ref[rows, cols].astype(f32) + both + bo[pl.ds(n * (TILE_N // 128) + i, 1), :]).astype(bf16)
        return carry

    lax.fori_loop(0, n_chunk * o_tiles, finish, 0)


def solution(mesh):
    n_cp = mesh.shape['cp']

    def local_block(hidden, seg_ids, w_q, b_q, w_kv, b_kv, w_o, b_o, ln_gain, ln_bias):
        tok, d_model = hidden.shape
        q_width = w_q.shape[1]
        n_chunk = tok // ROWS
        n_tiles = n_chunk * (d_model // TILE_N)
        vmem = pl.BlockSpec(memory_space=pltpu.VMEM)
        hbm = pl.BlockSpec(memory_space=pltpu.HBM)
        bf16, f32 = jnp.bfloat16, jnp.float32
        dma = pltpu.SemaphoreType.DMA
        flops = 2 * tok * d_model * (2 * q_width + 256)
        args = (hidden, seg_ids.reshape(-1, 128), w_q, b_q.reshape(-1, 128), w_kv, b_kv.reshape(-1, 128), w_o,
                b_o.reshape(-1, 128), ln_gain.reshape(-1, 128), ln_bias.reshape(-1, 128))
        args = tuple(pltpu.with_memory_space_constraint(a, pltpu.HBM) for a in args)
        rows = [q_width // 128, 2, d_model // 128, d_model // 128, d_model // 128]
        return pl.pallas_call(
            functools.partial(block_kernel, n_cp),
            out_shape=(pltpu.VMEM((tok, d_model), bf16), pltpu.VMEM((tok, HEAD_DIM), bf16), pltpu.VMEM((tok, HEAD_DIM), bf16)),
            in_specs=[hbm] * len(args),
            out_specs=(vmem, vmem, vmem),
            scratch_shapes=[
                pltpu.VMEM((tok, d_model), bf16),
                pltpu.VMEM((d_model, 2 * HEAD_DIM), bf16),
                pltpu.VMEM((SLOTS, TILE_K, TILE_N), bf16),
                pltpu.VMEM((n_cp, tok, 2 * HEAD_DIM), bf16),
                pltpu.VMEM((n_cp, tok // 128, 128), jnp.int32),
                pltpu.VMEM((ROWS, n_cp * tok), f32),
                pltpu.VMEM((ROWS, q_width), bf16),
                pltpu.VMEM((ROWS, q_width), bf16),
                pltpu.VMEM((n_tiles, ROWS, TILE_N), bf16),
                pltpu.VMEM((n_tiles, ROWS, TILE_N), bf16),
                *[pltpu.VMEM((r, 128), bf16) for r in rows],
                *[pltpu.VMEM((r, 128), f32) for r in rows],
                dma((tok // LN_ROWS,)), dma, dma((6,)), dma((SLOTS,)),
                dma((n_cp, n_chunk)), dma((n_cp, n_chunk)), dma((n_cp,)), dma((n_cp,)),
                dma((n_tiles,)), dma((n_tiles,)),
            ],
            compiler_params=pltpu.CompilerParams(collective_id=0, has_side_effects=True, vmem_limit_bytes=56 * 1024 * 1024),
            cost_estimate=pl.CostEstimate(flops=flops, bytes_accessed=2 * 4 * d_model * q_width, transcendentals=0),
        )(*args)

    row_spec = P(('dp', 'cp'), None)
    tok_spec = P(('dp', 'cp'))
    return jax.shard_map(local_block, mesh=mesh,
                         in_specs=(row_spec, tok_spec, P(None, 'tp'), P('tp'), P(None, None), P(None), P('tp', None), P(None), P(None), P(None)),
                         out_specs=(row_spec, row_spec, row_spec), check_vma=False)
```

time: 110 us -> 98.8 us (0.90)
  local copies, waits for them, and re-layouts: 11.7 us -> 2.92 us
  Pallas kernels: 96.9 us -> 95.1 us
    reshape x5 -> x0, local copies, waits for them, and re-layouts: 6.51 us -> none  [the longest x1 1.33 us: local_block(): b_o.reshape(1, -1)]
    unnamed x7 -> x3, local copies, waits for them, and re-layouts: 5.18 us -> 2.92 us
    pallas_call x1, Pallas kernels: 96.9 us -> 95.1 us  [local_block(): pl.pallas_call(functools.partial(block_kernel, n_cp), out_shape=(pltpu.VM...]
where the time goes in v2:
time: 98.8 us; the launch traced here: 98.7 us
  Pallas kernels  95.1 us (96%)
  local copies, waits for them, and re-layouts  2.92 us (3%)
    pallas_call x1, Pallas kernels, local_block(): pl.pallas_call(functools.partial(block_kernel, n_cp), out_shape=(pltpu.VM...  95.1 us
    unnamed x3, local copies, waits for them, and re-layouts  2.92 us

profile of v2, /device:TPU:2, one launch (start us, length us, event | category | flops | bytes accessed | tf_op | source)
XLA Modules:
  0.0 98.7 jit_solution(935438730371724927)
XLA Ops:
  0.6 95.1 %shard_map.121 = (bf16[256,6144]{1,0:T(8,128)(2,1)S(1)}, bf16[256,128]{1,0:T(8,128)(2,1)S(1)}, bf16[256,128]{1,0:T(8,128)(2,1)S(1)}) custom-call(bf16[256,6144]{1,0:T(8,128)(2,1)} %hid_hbm.1, s32[2,128]{1,0:T(2,128)} %bitcast.10, bf16[6144,3072]{1,0:T(8,128)(2,1)} %wq_hbm.1, bf16[24,128]{1,0:T(8,128)(2,1)} %bitcast.9, bf16[6144,256]{1,0:T(8,128)(2,1)} %wkv_hbm.1, ...), custom_call_target="tpu_custom_call" | custom-call | flops 20132659200 | bytes 150994944 | tf_op jit(solution)/shard_map/pallas_call | solution.py:299
  95.8 1.7 %copy.16 = bf16[256,6144]{1,0:T(8,128)(2,1)} copy(bf16[256,6144]{1,0:T(8,128)(2,1)S(1)} %get-tuple-element.3) | data formatting | bytes 6291456
  97.4 0.6 copy.17
  98.1 0.6 copy.18
